TPU v7x, 32 devices: a whole 2x2x4 slice. The times are simulated.
32 devices in a mesh: dp: 4 (over y, x), vocab: 8 (over z, core).
Axes of the slice: x: 2, y: 2, z: 4, core: 2. Of those that a mesh axis runs over, the one named last changes fastest.
Arguments:
- hidden: bfloat16 [2048, 5120], P(('dp', 'vocab')), may hold values from -100 to 100
- tokens: int32 [2048], P('dp'), may hold values from 0 to 9215
- old_weight: bfloat16 [9216, 5120], P('vocab'), may hold values from -1 to 1
- new_weight: bfloat16 [9216, 5120], P('dp', 'vocab'), may hold values from -6 to 6
Outputs:
- logprob: float32 [2048], P(('dp', 'vocab'))
- engine_weight: bfloat16 [9216, 5120], P('vocab')
All inputs are finite; a program needn't handle non-finite values.
Results may differ from a plain program's by a relative error of at most 0.001.
Values may be sent and summed in bfloat16 or wider, within the bound.
A program may use at most 128 MiB of HBM per device.

v0:
```python
import functools

import jax
import jax.numpy as jnp
from jax import lax
from jax.experimental import pallas as pl
from jax.experimental.pallas import tpu as pltpu
from jax.sharding import PartitionSpec as P

MESH = pl.DeviceIdType.MESH
STRIPE = 384


def pick(index, choices):
    value = jnp.int32(choices[0])
    for k in range(1, len(choices)):
        value = jnp.where(index == k, choices[k], value)
    return value


def nearest_first(count):
    return [sorted(range(count), key=lambda other: (abs(other - own), other)) for own in range(count)]


def exchange(
    replicas, ranks, tokens, hidden, old, new, pieces, logprob,
    gathered, weight, logits, stats, local_sem, weight_sem,
    line_send, line_recv, pair_send, pair_recv,
    spread_send, spread_recv, cube_send, cube_recv, stat_send, stat_recv,
):
    d = lax.axis_index("dp")
    v = lax.axis_index("vocab")
    owners = ranks // replicas
    groups = ranks // 2
    g, core = v // 2, v % 2
    own_rows = hidden.shape[0]
    vocab_rows = old.shape[0]
    part = vocab_rows // replicas
    half = (part // 2) // 16 * 16
    bits = replicas.bit_length() - 1

    def remote(src, dst, send, recv, device):
        return pltpu.make_async_remote_copy(
            src_ref=src, dst_ref=dst, send_sem=send, recv_sem=recv, device_id=device, device_id_type=MESH
        )

    def rows_of(rank):
        return gathered.at[pl.ds(pl.multiple_of(rank * own_rows, own_rows), own_rows), :]

    def line(group, step, source=None):
        slot = rows_of(2 * group + core)
        way = 0 if step > 0 else 1
        return remote(
            slot if source is None else source, slot, line_send.at[way, group], line_recv.at[way, group],
            (d, v + 2 * step),
        )

    def pair(group, source=None):
        slot = rows_of(2 * group + core)
        return remote(
            slot if source is None else source, slot, pair_send.at[group], pair_recv.at[group], (d, v + 1 - 2 * core)
        )

    def pair_arrival(group):
        slot = rows_of(2 * group + 1 - core)
        return remote(slot, slot, pair_send.at[group], pair_recv.at[group], (d, v + 1 - 2 * core))

    own_copy = pltpu.make_async_copy(hidden, rows_of(v), local_sem.at[0])
    own_copy.start()
    pl.when(g < groups - 1)(lambda: line(g, 1, hidden).start())
    pl.when(g > 0)(lambda: line(g, -1, hidden).start())
    pair(g, hidden).start()

    def line_step(step):
        def below():
            line(g - step, 1).wait_recv()
            pl.when(g < groups - 1)(lambda: line(g - step, 1).start())
            pair(g - step).start()

        def above():
            line(g + step, -1).wait_recv()
            pl.when(g > 0)(lambda: line(g + step, -1).start())
            pair(g + step).start()

        pl.when(g >= step)(below)
        pl.when(g + step < groups)(above)

    def spread(offset, owner, stay=False):
        target = d ^ offset
        source = new.at[pl.ds(pl.multiple_of(owner * vocab_rows + target * part, 16), part), :]
        slot = pieces.at[v, pl.ds(pl.multiple_of(target * part, 16), part), :]
        if stay:
            return pltpu.make_async_copy(source, slot, spread_recv.at[v])
        index = offset * owners + owner
        return remote(source, slot, spread_send.at[index], spread_recv.at[v], (target, d * owners + owner))

    def spread_start(offset, owner):
        if offset:
            spread(offset, owner).start()
        else:
            pl.when(d * owners + owner == v)(lambda: spread(offset, owner, stay=True).start())
            pl.when(d * owners + owner != v)(lambda: spread(offset, owner).start())

    def spread_sent(offset, owner):
        if offset:
            spread(offset, owner).wait_send()
        else:
            pl.when(d * owners + owner != v)(lambda: spread(offset, owner).wait_send())

    def spread_arrival(source):
        slot = pieces.at[source, pl.ds(pl.multiple_of(d * part, 16), part), :]
        pltpu.make_async_copy(slot, slot, spread_recv.at[source]).wait()

    def span(holder, which):
        first, length = {"all": (0, part), "low": (0, half), "high": (half, part - half)}[which]
        return pl.ds(pl.multiple_of(holder * part + first, 16), length)

    links = []
    for mask in range(replicas):
        for bit in range(bits):
            if mask >> bit & 1:
                continue
            if mask == 0:
                links.append((mask, bit, "all"))
                continue
            if bit > mask.bit_length() - 1:
                links.append((mask, bit, "low"))
            if bit < (mask & -mask).bit_length() - 1:
                links.append((mask, bit, "high"))

    def cube(source, index):
        mask, bit, which = links[index]
        slot = pieces.at[source, span(d ^ mask, which), :]
        return remote(slot, slot, cube_send.at[source, index], cube_recv.at[source, index], (d ^ (1 << bit), v))

    def cube_arrival(source, index):
        mask, bit, which = links[index]
        slot = pieces.at[source, span(d ^ mask ^ (1 << bit), which), :]
        remote(slot, slot, cube_send.at[source, index], cube_recv.at[source, index], (d ^ (1 << bit), v)).wait_recv()

    def cube_level(source, level):
        for index, (mask, bit, which) in enumerate(links):
            if mask.bit_count() == level - 1:
                cube_arrival(source, index)
                for onward, (held, _, wanted) in enumerate(links):
                    if held == mask | 1 << bit and which in ("all", wanted):
                        cube(source, onward).start()

    for offset in list(range(1, replicas)) + [0]:
        for owner in range(owners):
            spread_start(offset, owner)

    weight_copy = pltpu.make_async_copy(old, weight, weight_sem.at[0])
    weight_copy.start()

    table = nearest_first(groups)

    def sources(step):
        group = pick(g, [table[own][step] for own in range(groups)])
        return [2 * group, 2 * group + 1]

    def first_level(step):
        for source in sources(step):
            spread_arrival(source)
            for index, (mask, _, _) in enumerate(links):
                if mask == 0:
                    cube(source, index).start()

    def later_levels(step):
        for level in range(1, bits + 1):
            for source in sources(step):
                cube_level(source, level)

    def matmul():
        for group in range(groups):
            pair_arrival(group).wait_recv()
        own_copy.wait()
        weight_copy.wait()
        wanted = tokens[...] - v * vocab_rows
        count = gathered.shape[0]

        def stripe(index, carry):
            top, total, target = carry
            first = pl.multiple_of(index * STRIPE, STRIPE)
            logits[...] = lax.dot_general(
                weight[pl.ds(first, STRIPE), :], gathered[...], (((1,), (1,)), ((), ())),
                preferred_element_type=jnp.float32,
            )
            values = logits[...]
            higher = jnp.maximum(top, jnp.max(values, axis=0, keepdims=True))
            total = total * jnp.exp(top - higher) + jnp.sum(jnp.exp(values - higher), axis=0, keepdims=True)
            ids = lax.broadcasted_iota(jnp.int32, values.shape, 0) + first
            target = target + jnp.sum(jnp.where(ids == wanted, values, 0.0), axis=0, keepdims=True)
            return higher, total, target

        start = (
            jnp.full((1, count), -jnp.inf, jnp.float32),
            jnp.zeros((1, count), jnp.float32),
            jnp.zeros((1, count), jnp.float32),
        )
        top, total, target = lax.fori_loop(0, vocab_rows // STRIPE, stripe, start)
        stats[v] = jnp.concatenate([top, total, target, jnp.zeros((5, count), jnp.float32)], axis=0)

    def stat(offset):
        return remote(
            stats.at[v], stats.at[v], stat_send.at[offset], stat_recv.at[offset], (d, (v + offset) % ranks)
        )

    def stat_arrival(offset):
        source = (v + ranks - offset) % ranks
        remote(
            stats.at[source], stats.at[source], stat_send.at[offset], stat_recv.at[offset], (d, source)
        ).wait_recv()

    for step in range(groups):
        first_level(step)
        if step > 0:
            later_levels(step - 1)
        if step + 1 < groups:
            line_step(step + 1)
        if step == groups - 2:
            matmul()
    for offset in range(1, ranks):
        stat(offset).start()
    later_levels(groups - 1)
    for offset in range(1, ranks):
        stat_arrival(offset)
    top = stats[0, 0:1, :]
    for rank in range(1, ranks):
        top = jnp.maximum(top, stats[rank, 0:1, :])
    total = jnp.zeros_like(top)
    target = jnp.zeros_like(top)
    for rank in range(ranks):
        total += stats[rank, 1:2, :] * jnp.exp(stats[rank, 0:1, :] - top)
        target += stats[rank, 2:3, :]
    logprob[...] = target - top - jnp.log(total)

    for offset in range(1, ranks):
        stat(offset).wait_send()
    for offset in range(replicas):
        for owner in range(owners):
            spread_sent(offset, owner)
    for source in range(ranks):
        for index in range(len(links)):
            cube(source, index).wait_send()
    for group in range(groups):
        pl.when((group <= g) & (g < groups - 1))(lambda: line(group, 1).wait_send())
        pl.when((group >= g) & (g > 0))(lambda: line(group, -1).wait_send())
        pair(group).wait_send()


def assemble(pieces, whole, sem):
    cols = pieces.shape[2]
    copies = [
        pltpu.make_async_copy(pieces.at[source], whole.at[:, pl.ds(source * cols, cols)], sem.at[source])
        for source in range(pieces.shape[0])
    ]
    for copy in copies:
        copy.start()
    for copy in copies:
        copy.wait()


def on_device(hidden, tokens, old_weight, new_weight):
    ranks = lax.axis_size("vocab")
    replicas = lax.axis_size("dp")
    rank = lax.axis_index("vocab")
    own_rows, width = hidden.shape
    vocab_rows = old_weight.shape[0]
    cols = new_weight.shape[1]
    count = own_rows * ranks
    dtype = new_weight.dtype
    groups = ranks // 2
    owners = ranks // replicas
    bits = replicas.bit_length() - 1
    copies = sum(1 if mask == 0 else int(bit > mask.bit_length() - 1) + int(bit < (mask & -mask).bit_length() - 1)
                 for mask in range(replicas) for bit in range(bits) if not mask >> bit & 1)
    dma = pltpu.SemaphoreType.DMA
    anywhere = pl.BlockSpec(memory_space=pl.ANY)
    local = pl.BlockSpec(memory_space=pltpu.VMEM)
    pieces, logprob = pl.pallas_call(
        functools.partial(exchange, replicas, ranks),
        out_shape=(
            pltpu.VMEM((ranks, vocab_rows, cols), dtype),
            jax.ShapeDtypeStruct((1, count), jnp.float32),
        ),
        in_specs=[local, anywhere, anywhere, anywhere],
        out_specs=(local, local),
        scratch_shapes=[
            pltpu.VMEM((count, width), hidden.dtype),
            pltpu.VMEM((vocab_rows, width), old_weight.dtype),
            pltpu.VMEM((STRIPE, count), jnp.float32),
            pltpu.VMEM((ranks, 8, count), jnp.float32),
            dma((1,)), dma((1,)),
            dma((2, groups)), dma((2, groups)), dma((groups,)), dma((groups,)),
            dma((replicas * owners,)), dma((ranks,)),
            dma((ranks, copies)), dma((ranks, copies)),
            dma((ranks,)), dma((ranks,)),
        ],
        compiler_params=pltpu.CompilerParams(has_side_effects=True, vmem_limit_bytes=44 * 1024 * 1024),
        name="exchange",
    )(tokens.reshape(1, count), hidden, old_weight, new_weight)
    logprob = lax.dynamic_slice(logprob[0], (rank * own_rows,), (own_rows,))
    if cols % 128 == 0:
        engine_weight = pl.pallas_call(
            assemble,
            out_shape=jax.ShapeDtypeStruct((vocab_rows, ranks * cols), dtype),
            in_specs=[anywhere],
            out_specs=anywhere,
            scratch_shapes=[dma((ranks,))],
            compiler_params=pltpu.CompilerParams(vmem_limit_bytes=1024 * 1024),
            name="assemble",
        )(pieces)
    else:
        engine_weight = jnp.swapaxes(pieces, 0, 1).reshape(vocab_rows, ranks * cols)
    return (logprob, engine_weight)


def solution(mesh):
    return jax.shard_map(
        on_device,
        mesh=mesh,
        in_specs=(P(("dp", "vocab"), None), P("dp"), P("vocab", None), P("dp", "vocab")),
        out_specs=(P(("dp", "vocab")), P("vocab", None)),
        check_vma=False,
    )
```

profile of v0, /device:TPU:1, one launch (start us, length us, event | category | flops | bytes accessed | tf_op | source)
XLA Modules:
  0.0 304.7 jit_solution(1435534463635212319)
XLA Ops:
  0.6 298.5 %exchange.1 = (bf16[8,1152,640]{2,1,0:T(8,128)(2,1)S(1)}, f32[1,512]{1,0:T(1,128)}) custom-call(s32[1,512]{1,0:T(1,128)} %bitcast.3, bf16[64,5120]{1,0:T(8,128)(2,1)} %hidden.1, bf16[1152,5120]{1,0:T(8,128)(2,1)} %old.1, bf16[2304,640]{1,0:T(8,128)(2,1)} %new.1), custom_call_target="tpu_custom_call" | custom-call | tf_op jit(solution)/shard_map/exchange/pallas_call | solution.py:281
  299.1 1.2 dynamic-slice_bitcast_fusion
  300.3 4.4 %assemble.1 = bf16[1152,5120]{1,0:T(8,128)(2,1)} custom-call(bf16[8,1152,640]{2,1,0:T(8,128)(2,1)S(1)} %get-tuple-element.5.pieces), custom_call_target="tpu_custom_call" | custom-call | tf_op jit(solution)/shard_map/assemble/pallas_call | solution.py:305
where the time goes:
time: 307 us; the launch traced here: 305 us
  Pallas kernels  303 us (99%)
    pallas_call x1, Pallas kernels, on_device(): pl.pallas_call(functools.partial(exchange, replicas, ranks), out_shape=(p...  299 us

commit v1 on v0

--- a/solution.py
+++ b/solution.py
@@ -24,8 +24,8 @@
 
 def exchange(
     replicas, ranks, tokens, hidden, old, new, pieces, logprob,
-    gathered, weight, logits, stats, local_sem, weight_sem,
-    line_send, line_recv, pair_send, pair_recv,
+    gathered, weight, logits, stats, relay, local_sem, weight_sem,
+    line_send, line_recv, pair_send, pair_recv, relay_send, relay_recv,
     spread_send, spread_recv, cube_send, cube_recv, stat_send, stat_recv,
 ):
     d = lax.axis_index("dp")
@@ -85,27 +85,32 @@
         pl.when(g >= step)(below)
         pl.when(g + step < groups)(above)
 
-    def spread(offset, owner, stay=False):
+    def hand(offset, owner):
         target = d ^ offset
         source = new.at[pl.ds(pl.multiple_of(owner * vocab_rows + target * part, 16), part), :]
-        slot = pieces.at[v, pl.ds(pl.multiple_of(target * part, 16), part), :]
+        slot = relay.at[offset - 1, owner]
+        index = (offset - 1) * owners + owner
+        return remote(source, slot, relay_send.at[index], relay_recv.at[index], (target, v))
+
+    def spread(offset, owner, stay=False):
+        rank = (d ^ offset) * owners + owner
+        if offset:
+            source = relay.at[offset - 1, owner]
+        else:
+            source = new.at[pl.ds(pl.multiple_of(owner * vocab_rows + d * part, 16), part), :]
+        slot = pieces.at[v, pl.ds(pl.multiple_of(d * part, 16), part), :]
         if stay:
             return pltpu.make_async_copy(source, slot, spread_recv.at[v])
-        index = offset * owners + owner
-        return remote(source, slot, spread_send.at[index], spread_recv.at[v], (target, d * owners + owner))
+        return remote(source, slot, spread_send.at[offset * owners + owner], spread_recv.at[v], (d, rank))
 
     def spread_start(offset, owner):
-        if offset:
-            spread(offset, owner).start()
-        else:
-            pl.when(d * owners + owner == v)(lambda: spread(offset, owner, stay=True).start())
-            pl.when(d * owners + owner != v)(lambda: spread(offset, owner).start())
+        rank = (d ^ offset) * owners + owner
+        pl.when(rank == v)(lambda: spread(offset, owner, stay=True).start())
+        pl.when(rank != v)(lambda: spread(offset, owner).start())
 
     def spread_sent(offset, owner):
-        if offset:
-            spread(offset, owner).wait_send()
-        else:
-            pl.when(d * owners + owner != v)(lambda: spread(offset, owner).wait_send())
+        rank = (d ^ offset) * owners + owner
+        pl.when(rank != v)(lambda: spread(offset, owner).wait_send())
 
     def spread_arrival(source):
         slot = pieces.at[source, pl.ds(pl.multiple_of(d * part, 16), part), :]
@@ -146,9 +151,11 @@
                     if held == mask | 1 << bit and which in ("all", wanted):
                         cube(source, onward).start()
 
-    for offset in list(range(1, replicas)) + [0]:
+    for offset in range(1, replicas):
         for owner in range(owners):
-            spread_start(offset, owner)
+            hand(offset, owner).start()
+    for owner in range(owners):
+        spread_start(0, owner)
 
     weight_copy = pltpu.make_async_copy(old, weight, weight_sem.at[0])
     weight_copy.start()
@@ -212,6 +219,10 @@
             stats.at[source], stats.at[source], stat_send.at[offset], stat_recv.at[offset], (d, source)
         ).wait_recv()
 
+    for offset in range(1, replicas):
+        for owner in range(owners):
+            hand(offset, owner).wait_recv()
+            spread_start(offset, owner)
     for step in range(groups):
         first_level(step)
         if step > 0:
@@ -240,6 +251,8 @@
     for offset in range(replicas):
         for owner in range(owners):
             spread_sent(offset, owner)
+            if offset:
+                hand(offset, owner).wait_send()
     for source in range(ranks):
         for index in range(len(links)):
             cube(source, index).wait_send()
@@ -291,8 +304,10 @@
             pltpu.VMEM((vocab_rows, width), old_weight.dtype),
             pltpu.VMEM((STRIPE, count), jnp.float32),
             pltpu.VMEM((ranks, 8, count), jnp.float32),
+            pltpu.VMEM((replicas - 1, owners, vocab_rows // replicas, cols), dtype),
             dma((1,)), dma((1,)),
             dma((2, groups)), dma((2, groups)), dma((groups,)), dma((groups,)),
+            dma(((replicas - 1) * owners,)), dma(((replicas - 1) * owners,)),
             dma((replicas * owners,)), dma((ranks,)),
             dma((ranks, copies)), dma((ranks, copies)),
             dma((ranks,)), dma((ranks,)),

time: 307 us -> 180 us (0.59)
  the two profiles are of different devices: /device:TPU:1 before, /device:TPU:17 now
where the time goes in v1:
time: 180 us
  Pallas kernels  178 us (99%)
    pallas_call x1, Pallas kernels, on_device(): pl.pallas_call(functools.partial(exchange, replicas, ranks), out_shape=(p...  174 us
    pallas_call x1, Pallas kernels, on_device(): pl.pallas_call(assemble, out_shape=jax.ShapeDtypeStruct((vocab_rows, rank...  4.41 us

profile of v1, /device:TPU:17, one launch (start us, length us, event | category | flops | bytes accessed | tf_op | source)
XLA Modules:
  0.0 180.3 jit_solution(14945098965117124583)
XLA Ops:
  0.6 174.0 %exchange.1 = (bf16[8,1152,640]{2,1,0:T(8,128)(2,1)S(1)}, f32[1,512]{1,0:T(1,128)}) custom-call(s32[1,512]{1,0:T(1,128)} %bitcast.3, bf16[64,5120]{1,0:T(8,128)(2,1)} %hidden.1, bf16[1152,5120]{1,0:T(8,128)(2,1)} %old.1, bf16[2304,640]{1,0:T(8,128)(2,1)} %new.1), custom_call_target="tpu_custom_call" | custom-call | tf_op jit(solution)/shard_map/exchange/pallas_call | solution.py:294
  174.6 1.3 dynamic-slice_bitcast_fusion
  175.9 4.4 %assemble.1 = bf16[1152,5120]{1,0:T(8,128)(2,1)} custom-call(bf16[8,1152,640]{2,1,0:T(8,128)(2,1)S(1)} %get-tuple-element.5.pieces), custom_call_target="tpu_custom_call" | custom-call | tf_op jit(solution)/shard_map/assemble/pallas_call | solution.py:320

commit v2 on v1

--- a/solution.py
+++ b/solution.py
@@ -11,15 +11,13 @@
 STRIPE = 384
 
 
-def pick(index, choices):
-    value = jnp.int32(choices[0])
-    for k in range(1, len(choices)):
-        value = jnp.where(index == k, choices[k], value)
-    return value
-
-
-def nearest_first(count):
-    return [sorted(range(count), key=lambda other: (abs(other - own), other)) for own in range(count)]
+def plan_of(replicas, groups, stripes):
+    tasks = [("hand", offset) for offset in range(1, replicas)] + [("line", 0)]
+    tasks += [("spread", turn) for turn in range(groups)] + [("first", 0)]
+    for turn in range(1, groups):
+        tasks += [("first", turn), ("later", turn - 1), ("line", turn)]
+    tasks += [("logits", stripe) for stripe in range(stripes)]
+    return tasks + [("stats", 0), ("later", groups - 1)]
 
 
 def exchange(
@@ -66,12 +64,19 @@
         return remote(slot, slot, pair_send.at[group], pair_recv.at[group], (d, v + 1 - 2 * core))
 
     own_copy = pltpu.make_async_copy(hidden, rows_of(v), local_sem.at[0])
-    own_copy.start()
-    pl.when(g < groups - 1)(lambda: line(g, 1, hidden).start())
-    pl.when(g > 0)(lambda: line(g, -1, hidden).start())
-    pair(g, hidden).start()
+    weight_copy = pltpu.make_async_copy(old, weight, weight_sem.at[0])
+
+    def line_start():
+        pl.when(g < groups - 1)(lambda: line(g, 1, hidden).start())
+        pl.when(g > 0)(lambda: line(g, -1, hidden).start())
+        pair(g, hidden).start()
+        own_copy.start()
+        weight_copy.start()
 
     def line_step(step):
+        if step == 0:
+            return line_start()
+
         def below():
             line(g - step, 1).wait_recv()
             pl.when(g < groups - 1)(lambda: line(g - step, 1).start())
@@ -92,25 +97,43 @@
         index = (offset - 1) * owners + owner
         return remote(source, slot, relay_send.at[index], relay_recv.at[index], (target, v))
 
-    def spread(offset, owner, stay=False):
-        rank = (d ^ offset) * owners + owner
-        if offset:
-            source = relay.at[offset - 1, owner]
-        else:
-            source = new.at[pl.ds(pl.multiple_of(owner * vocab_rows + d * part, 16), part), :]
+    def spread(turn, owner, source, stay=False):
         slot = pieces.at[v, pl.ds(pl.multiple_of(d * part, 16), part), :]
         if stay:
             return pltpu.make_async_copy(source, slot, spread_recv.at[v])
-        return remote(source, slot, spread_send.at[offset * owners + owner], spread_recv.at[v], (d, rank))
-
-    def spread_start(offset, owner):
-        rank = (d ^ offset) * owners + owner
-        pl.when(rank == v)(lambda: spread(offset, owner, stay=True).start())
-        pl.when(rank != v)(lambda: spread(offset, owner).start())
-
-    def spread_sent(offset, owner):
-        rank = (d ^ offset) * owners + owner
-        pl.when(rank != v)(lambda: spread(offset, owner).wait_send())
+        rank = (g ^ turn) * owners + owner
+        return remote(source, slot, spread_send.at[turn * owners + owner], spread_recv.at[v], (d, rank))
+
+    def spread_from(turn, owner, source):
+        if turn:
+            return spread(turn, owner, source).start()
+        pl.when(owner == core)(lambda: spread(turn, owner, source, stay=True).start())
+        pl.when(owner != core)(lambda: spread(turn, owner, source).start())
+
+    def spread_turn(turn):
+        offset = d ^ g ^ turn
+
+        def own():
+            for owner in range(owners):
+                first = pl.multiple_of(owner * vocab_rows + d * part, 16)
+                spread_from(turn, owner, new.at[pl.ds(first, part), :])
+
+        def handed():
+            for owner in range(owners):
+                hand(offset, owner).wait_recv()
+                spread_from(turn, owner, relay.at[offset - 1, owner])
+
+        pl.when(offset == 0)(own)
+        pl.when(offset != 0)(handed)
+
+    def spread_sent(turn, owner):
+        def sent():
+            spread(turn, owner, relay.at[0, owner]).wait_send()
+
+        if turn:
+            sent()
+        else:
+            pl.when(owner != core)(sent)
 
     def spread_arrival(source):
         slot = pieces.at[source, pl.ds(pl.multiple_of(d * part, 16), part), :]
@@ -151,20 +174,8 @@
                     if held == mask | 1 << bit and which in ("all", wanted):
                         cube(source, onward).start()
 
-    for offset in range(1, replicas):
-        for owner in range(owners):
-            hand(offset, owner).start()
-    for owner in range(owners):
-        spread_start(0, owner)
-
-    weight_copy = pltpu.make_async_copy(old, weight, weight_sem.at[0])
-    weight_copy.start()
-
-    table = nearest_first(groups)
-
-    def sources(step):
-        group = pick(g, [table[own][step] for own in range(groups)])
-        return [2 * group, 2 * group + 1]
+    def sources(turn):
+        return [2 * (g ^ turn), 2 * (g ^ turn) + 1]
 
     def first_level(step):
         for source in sources(step):
@@ -174,39 +185,34 @@
                     cube(source, index).start()
 
     def later_levels(step):
-        for level in range(1, bits + 1):
+        for level in range(1, bits):
             for source in sources(step):
                 cube_level(source, level)
 
-    def matmul():
-        for group in range(groups):
-            pair_arrival(group).wait_recv()
-        own_copy.wait()
-        weight_copy.wait()
-        wanted = tokens[...] - v * vocab_rows
+    def logits_stripe(index):
         count = gathered.shape[0]
-
-        def stripe(index, carry):
-            top, total, target = carry
-            first = pl.multiple_of(index * STRIPE, STRIPE)
-            logits[...] = lax.dot_general(
-                weight[pl.ds(first, STRIPE), :], gathered[...], (((1,), (1,)), ((), ())),
-                preferred_element_type=jnp.float32,
-            )
-            values = logits[...]
-            higher = jnp.maximum(top, jnp.max(values, axis=0, keepdims=True))
-            total = total * jnp.exp(top - higher) + jnp.sum(jnp.exp(values - higher), axis=0, keepdims=True)
-            ids = lax.broadcasted_iota(jnp.int32, values.shape, 0) + first
-            target = target + jnp.sum(jnp.where(ids == wanted, values, 0.0), axis=0, keepdims=True)
-            return higher, total, target
-
-        start = (
-            jnp.full((1, count), -jnp.inf, jnp.float32),
-            jnp.zeros((1, count), jnp.float32),
-            jnp.zeros((1, count), jnp.float32),
-        )
-        top, total, target = lax.fori_loop(0, vocab_rows // STRIPE, stripe, start)
-        stats[v] = jnp.concatenate([top, total, target, jnp.zeros((5, count), jnp.float32)], axis=0)
+        if index == 0:
+            for group in range(groups):
+                pair_arrival(group).wait_recv()
+            own_copy.wait()
+            weight_copy.wait()
+            floor = jnp.full((1, count), -jnp.inf, jnp.float32)
+            stats[v] = jnp.concatenate([floor, jnp.zeros((7, count), jnp.float32)], axis=0)
+        first = index * STRIPE
+        logits[...] = lax.dot_general(
+            weight[pl.ds(first, STRIPE), :], gathered[...], (((1,), (1,)), ((), ())),
+            preferred_element_type=jnp.float32,
+        )
+        values = logits[...]
+        top = stats[v, 0:1, :]
+        higher = jnp.maximum(top, jnp.max(values, axis=0, keepdims=True))
+        total = stats[v, 1:2, :] * jnp.exp(top - higher)
+        total += jnp.sum(jnp.exp(values - higher), axis=0, keepdims=True)
+        ids = lax.broadcasted_iota(jnp.int32, values.shape, 0) + (first + v * vocab_rows)
+        target = jnp.sum(jnp.where(ids == tokens[...], values, 0.0), axis=0, keepdims=True)
+        stats[v, 0:1, :] = higher
+        stats[v, 1:2, :] = total
+        stats[v, 2:3, :] += target
 
     def stat(offset):
         return remote(
@@ -219,21 +225,22 @@
             stats.at[source], stats.at[source], stat_send.at[offset], stat_recv.at[offset], (d, source)
         ).wait_recv()
 
-    for offset in range(1, replicas):
+    def hand_start(offset):
         for owner in range(owners):
-            hand(offset, owner).wait_recv()
-            spread_start(offset, owner)
-    for step in range(groups):
-        first_level(step)
-        if step > 0:
-            later_levels(step - 1)
-        if step + 1 < groups:
-            line_step(step + 1)
-        if step == groups - 2:
-            matmul()
-    for offset in range(1, ranks):
-        stat(offset).start()
-    later_levels(groups - 1)
+            hand(offset, owner).start()
+
+    def stats_start(_):
+        for offset in range(1, ranks):
+            stat(offset).start()
+
+    run = {
+        "hand": hand_start, "line": line_step, "spread": spread_turn, "first": first_level,
+        "later": later_levels, "logits": logits_stripe, "stats": stats_start,
+    }
+    for task, index in plan_of(replicas, groups, vocab_rows // STRIPE):
+        run[task](index)
+    for source in range(ranks):
+        cube_level(source, bits)
     for offset in range(1, ranks):
         stat_arrival(offset)
     top = stats[0, 0:1, :]
@@ -248,11 +255,11 @@
 
     for offset in range(1, ranks):
         stat(offset).wait_send()
-    for offset in range(replicas):
-        for owner in range(owners):
-            spread_sent(offset, owner)
-            if offset:
-                hand(offset, owner).wait_send()
+    for owner in range(owners):
+        for turn in range(groups):
+            spread_sent(turn, owner)
+        for offset in range(1, replicas):
+            hand(offset, owner).wait_send()
     for source in range(ranks):
         for index in range(len(links)):
             cube(source, index).wait_send()
@@ -285,6 +292,7 @@
     dtype = new_weight.dtype
     groups = ranks // 2
     owners = ranks // replicas
+    assert groups == replicas == 1 << (replicas.bit_length() - 1)
     bits = replicas.bit_length() - 1
     copies = sum(1 if mask == 0 else int(bit > mask.bit_length() - 1) + int(bit < (mask & -mask).bit_length() - 1)
                  for mask in range(replicas) for bit in range(bits) if not mask >> bit & 1)
@@ -308,7 +316,7 @@
             dma((1,)), dma((1,)),
             dma((2, groups)), dma((2, groups)), dma((groups,)), dma((groups,)),
             dma(((replicas - 1) * owners,)), dma(((replicas - 1) * owners,)),
-            dma((replicas * owners,)), dma((ranks,)),
+            dma((groups * owners,)), dma((ranks,)),
             dma((ranks, copies)), dma((ranks, copies)),
             dma((ranks,)), dma((ranks,)),
         ],

time: 180 us -> 164 us (0.911)
  the two profiles are of different devices: /device:TPU:17 before, /device:TPU:1 now
where the time goes in v2:
time: 164 us
  Pallas kernels  162 us (99%)
    pallas_call x1, Pallas kernels, on_device(): pl.pallas_call(functools.partial(exchange, replicas, ranks), out_shape=(p...  158 us
    pallas_call x1, Pallas kernels, on_device(): pl.pallas_call(assemble, out_shape=jax.ShapeDtypeStruct((vocab_rows, rank...  4.41 us

profile of v2, /device:TPU:1, one launch (start us, length us, event | category | flops | bytes accessed | tf_op | source)
XLA Modules:
  0.0 163.9 jit_solution(11018423607589945106)
XLA Ops:
  0.6 157.7 %exchange.1 = (bf16[8,1152,640]{2,1,0:T(8,128)(2,1)S(1)}, f32[1,512]{1,0:T(1,128)}) custom-call(s32[1,512]{1,0:T(1,128)} %bitcast.3, bf16[64,5120]{1,0:T(8,128)(2,1)} %hidden.1, bf16[1152,5120]{1,0:T(8,128)(2,1)} %old.1, bf16[2304,640]{1,0:T(8,128)(2,1)} %new.1), custom_call_target="tpu_custom_call" | custom-call | tf_op jit(solution)/shard_map/exchange/pallas_call | solution.py:302
  158.3 1.2 dynamic-slice_bitcast_fusion
  159.5 4.4 %assemble.1 = bf16[1152,5120]{1,0:T(8,128)(2,1)} custom-call(bf16[8,1152,640]{2,1,0:T(8,128)(2,1)S(1)} %get-tuple-element.5.pieces), custom_call_target="tpu_custom_call" | custom-call | tf_op jit(solution)/shard_map/assemble/pallas_call | solution.py:328

commit v3 on v2

--- a/solution.py
+++ b/solution.py
@@ -12,10 +12,12 @@
 
 
 def plan_of(replicas, groups, stripes):
-    tasks = [("hand", offset) for offset in range(1, replicas)] + [("line", 0)]
-    tasks += [("spread", turn) for turn in range(groups)] + [("first", 0)]
-    for turn in range(1, groups):
-        tasks += [("first", turn), ("later", turn - 1), ("line", turn)]
+    tasks = [("hand", 2), ("line", 0), ("hand", 1)] + [("hand", offset) for offset in range(3, replicas)]
+    tasks += [("line", 1), ("spread", 1), ("spread", 2), ("spread", 0)]
+    tasks += [("spread", turn) for turn in range(3, groups)]
+    tasks += [("first", 0), ("later", 0), ("first", 1), ("first", 2), ("line", 2), ("later", 1), ("later", 2)]
+    for turn in range(3, groups):
+        tasks += [("later", turn - 1)] * (turn > 3) + [("line", turn), ("first", turn)]
     tasks += [("logits", stripe) for stripe in range(stripes)]
     return tasks + [("stats", 0), ("later", groups - 1)]
 

time: 164 us -> 149 us (0.909)
  Pallas kernels: 162 us -> 147 us
    pallas_call x1, Pallas kernels: 158 us -> 142 us  [on_device(): pl.pallas_call(functools.partial(exchange, replicas, ranks), out_shape=(p...]
where the time goes in v3:
time: 149 us; the launch traced here: 148 us
  Pallas kernels  147 us (99%)
    pallas_call x1, Pallas kernels, on_device(): pl.pallas_call(functools.partial(exchange, replicas, ranks), out_shape=(p...  142 us
    pallas_call x1, Pallas kernels, on_device(): pl.pallas_call(assemble, out_shape=jax.ShapeDtypeStruct((vocab_rows, rank...  4.41 us

profile of v3, /device:TPU:1, one launch (start us, length us, event | category | flops | bytes accessed | tf_op | source)
XLA Modules:
  0.0 148.5 jit_solution(1649376783990229766)
XLA Ops:
  0.6 142.3 %exchange.1 = (bf16[8,1152,640]{2,1,0:T(8,128)(2,1)S(1)}, f32[1,512]{1,0:T(1,128)}) custom-call(s32[1,512]{1,0:T(1,128)} %bitcast.3, bf16[64,5120]{1,0:T(8,128)(2,1)} %hidden.1, bf16[1152,5120]{1,0:T(8,128)(2,1)} %old.1, bf16[2304,640]{1,0:T(8,128)(2,1)} %new.1), custom_call_target="tpu_custom_call" | custom-call | tf_op jit(solution)/shard_map/exchange/pallas_call | solution.py:304
  142.9 1.2 dynamic-slice_bitcast_fusion
  144.1 4.4 %assemble.1 = bf16[1152,5120]{1,0:T(8,128)(2,1)} custom-call(bf16[8,1152,640]{2,1,0:T(8,128)(2,1)S(1)} %get-tuple-element.5.pieces), custom_call_target="tpu_custom_call" | custom-call | tf_op jit(solution)/shard_map/assemble/pallas_call | solution.py:330

commit v4 on v3

--- a/solution.py
+++ b/solution.py
@@ -65,6 +65,12 @@
         slot = rows_of(2 * group + 1 - core)
         return remote(slot, slot, pair_send.at[group], pair_recv.at[group], (d, v + 1 - 2 * core))
 
+    ready = pltpu.get_barrier_semaphore()
+    for offset in range(1, replicas):
+        pl.semaphore_signal(ready, inc=1, device_id=(d ^ offset, v), device_id_type=MESH)
+    for offset in range(1, ranks):
+        pl.semaphore_signal(ready, inc=1, device_id=(d, (v + offset) % ranks), device_id_type=MESH)
+
     own_copy = pltpu.make_async_copy(hidden, rows_of(v), local_sem.at[0])
     weight_copy = pltpu.make_async_copy(old, weight, weight_sem.at[0])
 
@@ -72,8 +78,6 @@
         pl.when(g < groups - 1)(lambda: line(g, 1, hidden).start())
         pl.when(g > 0)(lambda: line(g, -1, hidden).start())
         pair(g, hidden).start()
-        own_copy.start()
-        weight_copy.start()
 
     def line_step(step):
         if step == 0:
@@ -239,6 +243,9 @@
         "hand": hand_start, "line": line_step, "spread": spread_turn, "first": first_level,
         "later": later_levels, "logits": logits_stripe, "stats": stats_start,
     }
+    own_copy.start()
+    weight_copy.start()
+    pl.semaphore_wait(ready, replicas + ranks - 2)
     for task, index in plan_of(replicas, groups, vocab_rows // STRIPE):
         run[task](index)
     for source in range(ranks):
@@ -253,7 +260,10 @@
     for rank in range(ranks):
         total += stats[rank, 1:2, :] * jnp.exp(stats[rank, 0:1, :] - top)
         target += stats[rank, 2:3, :]
-    logprob[...] = target - top - jnp.log(total)
+    result = target - top - jnp.log(total)
+    for rank in range(ranks):
+        own = result[:, rank * own_rows : (rank + 1) * own_rows]
+        pl.when(v == rank)(lambda: logprob.__setitem__((slice(0, 1), slice(0, own_rows)), own))
 
     for offset in range(1, ranks):
         stat(offset).wait_send()
@@ -271,7 +281,7 @@
         pair(group).wait_send()
 
 
-def assemble(pieces, whole, sem):
+def assemble(pieces, result, whole, logprob, sem):
     cols = pieces.shape[2]
     copies = [
         pltpu.make_async_copy(pieces.at[source], whole.at[:, pl.ds(source * cols, cols)], sem.at[source])
@@ -279,6 +289,7 @@
     ]
     for copy in copies:
         copy.start()
+    logprob[...] = result[...]
     for copy in copies:
         copy.wait()
 
@@ -286,7 +297,6 @@
 def on_device(hidden, tokens, old_weight, new_weight):
     ranks = lax.axis_size("vocab")
     replicas = lax.axis_size("dp")
-    rank = lax.axis_index("vocab")
     own_rows, width = hidden.shape
     vocab_rows = old_weight.shape[0]
     cols = new_weight.shape[1]
@@ -305,7 +315,7 @@
         functools.partial(exchange, replicas, ranks),
         out_shape=(
             pltpu.VMEM((ranks, vocab_rows, cols), dtype),
-            jax.ShapeDtypeStruct((1, count), jnp.float32),
+            pltpu.VMEM((1, own_rows), jnp.float32),
         ),
         in_specs=[local, anywhere, anywhere, anywhere],
         out_specs=(local, local),
@@ -322,23 +332,27 @@
             dma((ranks, copies)), dma((ranks, copies)),
             dma((ranks,)), dma((ranks,)),
         ],
-        compiler_params=pltpu.CompilerParams(has_side_effects=True, vmem_limit_bytes=44 * 1024 * 1024),
+        compiler_params=pltpu.CompilerParams(
+            collective_id=0, has_side_effects=True, vmem_limit_bytes=44 * 1024 * 1024
+        ),
         name="exchange",
     )(tokens.reshape(1, count), hidden, old_weight, new_weight)
-    logprob = lax.dynamic_slice(logprob[0], (rank * own_rows,), (own_rows,))
     if cols % 128 == 0:
-        engine_weight = pl.pallas_call(
+        engine_weight, logprob = pl.pallas_call(
             assemble,
-            out_shape=jax.ShapeDtypeStruct((vocab_rows, ranks * cols), dtype),
-            in_specs=[anywhere],
-            out_specs=anywhere,
+            out_shape=(
+                jax.ShapeDtypeStruct((vocab_rows, ranks * cols), dtype),
+                jax.ShapeDtypeStruct((1, own_rows), jnp.float32),
+            ),
+            in_specs=[anywhere, local],
+            out_specs=(anywhere, local),
             scratch_shapes=[dma((ranks,))],
             compiler_params=pltpu.CompilerParams(vmem_limit_bytes=1024 * 1024),
             name="assemble",
-        )(pieces)
+        )(pieces, logprob)
     else:
         engine_weight = jnp.swapaxes(pieces, 0, 1).reshape(vocab_rows, ranks * cols)
-    return (logprob, engine_weight)
+    return (logprob.reshape(own_rows), engine_weight)
 
 
 def solution(mesh):

time: 149 us -> 145 us (0.973)
  Pallas kernels: 147 us -> 144 us
    pallas_call x1, Pallas kernels: 142 us -> 139 us  [on_device(): pl.pallas_call(functools.partial(exchange, replicas, ranks), out_shape=(p...]
where the time goes in v4:
time: 145 us; the launch traced here: 144 us
  Pallas kernels  144 us (99%)
    pallas_call x1, Pallas kernels, on_device(): pl.pallas_call(functools.partial(exchange, replicas, ranks), out_shape=(p...  139 us
    pallas_call x1, Pallas kernels, on_device(): pl.pallas_call(assemble, out_shape=(jax.ShapeDtypeStruct((vocab_rows, ran...  4.92 us

profile of v4, /device:TPU:1, one launch (start us, length us, event | category | flops | bytes accessed | tf_op | source)
XLA Modules:
  0.0 144.4 jit_solution(8400725358110581336)
XLA Ops:
  0.6 138.8 %exchange.1 = (bf16[8,1152,640]{2,1,0:T(8,128)(2,1)S(1)}, f32[1,64]{1,0:T(1,128)S(1)}) custom-call(s32[1,512]{1,0:T(1,128)} %bitcast.2, bf16[64,5120]{1,0:T(8,128)(2,1)} %hidden.1, bf16[1152,5120]{1,0:T(8,128)(2,1)} %old.1, bf16[2304,640]{1,0:T(8,128)(2,1)} %new.1), custom_call_target="tpu_custom_call" | custom-call | tf_op jit(solution)/shard_map/exchange/pallas_call | solution.py:314
  139.5 4.9 %assemble.1 = (bf16[1152,5120]{1,0:T(8,128)(2,1)}, f32[1,64]{1,0:T(1,128)}) custom-call(bf16[8,1152,640]{2,1,0:T(8,128)(2,1)S(1)} %get-tuple-element.6.pieces, f32[1,64]{1,0:T(1,128)S(1)} %get-tuple-element.7.result), custom_call_target="tpu_custom_call" | custom-call | tf_op jit(solution)/shard_map/assemble/pallas_call | solution.py:341

commit v5 on v4

--- a/solution.py
+++ b/solution.py
@@ -116,16 +116,19 @@
         pl.when(owner == core)(lambda: spread(turn, owner, source, stay=True).start())
         pl.when(owner != core)(lambda: spread(turn, owner, source).start())
 
+    def in_turn():
+        return [lax.rem(core + k, owners) for k in range(owners)]
+
     def spread_turn(turn):
         offset = d ^ g ^ turn
 
         def own():
-            for owner in range(owners):
+            for owner in in_turn():
                 first = pl.multiple_of(owner * vocab_rows + d * part, 16)
                 spread_from(turn, owner, new.at[pl.ds(first, part), :])
 
         def handed():
-            for owner in range(owners):
+            for owner in in_turn():
                 hand(offset, owner).wait_recv()
                 spread_from(turn, owner, relay.at[offset - 1, owner])
 
@@ -181,7 +184,7 @@
                         cube(source, onward).start()
 
     def sources(turn):
-        return [2 * (g ^ turn), 2 * (g ^ turn) + 1]
+        return [2 * (g ^ turn) + core, 2 * (g ^ turn) + 1 - core]
 
     def first_level(step):
         for source in sources(step):
@@ -232,7 +235,7 @@
         ).wait_recv()
 
     def hand_start(offset):
-        for owner in range(owners):
+        for owner in in_turn():
             hand(offset, owner).start()
 
     def stats_start(_):

time: 145 us -> 144 us (level)
  Pallas kernels: 144 us -> 142 us
    pallas_call x1, Pallas kernels: 139 us -> 137 us  [on_device(): pl.pallas_call(functools.partial(exchange, replicas, ranks), out_shape=(p...]
where the time goes in v5:
time: 144 us; the launch traced here: 142 us
  Pallas kernels  142 us (99%)
    pallas_call x1, Pallas kernels, on_device(): pl.pallas_call(functools.partial(exchange, replicas, ranks), out_shape=(p...  137 us
    pallas_call x1, Pallas kernels, on_device(): pl.pallas_call(assemble, out_shape=(jax.ShapeDtypeStruct((vocab_rows, ran...  4.92 us

profile of v5, /device:TPU:1, one launch (start us, length us, event | category | flops | bytes accessed | tf_op | source)
XLA Modules:
  0.0 142.4 jit_solution(1719718615898837404)
XLA Ops:
  0.6 136.8 %exchange.1 = (bf16[8,1152,640]{2,1,0:T(8,128)(2,1)S(1)}, f32[1,64]{1,0:T(1,128)S(1)}) custom-call(s32[1,512]{1,0:T(1,128)} %bitcast.2, bf16[64,5120]{1,0:T(8,128)(2,1)} %hidden.1, bf16[1152,5120]{1,0:T(8,128)(2,1)} %old.1, bf16[2304,640]{1,0:T(8,128)(2,1)} %new.1), custom_call_target="tpu_custom_call" | custom-call | tf_op jit(solution)/shard_map/exchange/pallas_call | solution.py:317
  137.5 4.9 %assemble.1 = (bf16[1152,5120]{1,0:T(8,128)(2,1)}, f32[1,64]{1,0:T(1,128)}) custom-call(bf16[8,1152,640]{2,1,0:T(8,128)(2,1)S(1)} %get-tuple-element.6.pieces, f32[1,64]{1,0:T(1,128)S(1)} %get-tuple-element.7.result), custom_call_target="tpu_custom_call" | custom-call | tf_op jit(solution)/shard_map/assemble/pallas_call | solution.py:344
